TPU v7x, 32 devices: a whole 2x2x4 slice. The times are simulated.
32 devices in a mesh: dp: 8 (over z, x), param: 4 (over y, core).
Axes of the slice: x: 2, y: 2, z: 4, core: 2. Of those that a mesh axis runs over, the one named last changes fastest.
Arguments:
- ex_grads: bfloat16 [768, 5120], P('dp', 'param'), may hold values from -6 to 6
- tgt_grads: bfloat16 [2048, 5120], P('dp', 'param'), may hold values from -6 to 6
- projection: bfloat16 [5120, 4096], P('param'), may hold values from -0.078125 to 0.078125
- example_weight: float32 [768], P('param'), may hold values from 0.05 to 1
Outputs:
- scores: float32 [2048, 768], P('dp', 'param')
All inputs are finite; a program needn't handle non-finite values.
Results may differ from a plain program's by a relative error of at most 0.0078.
Values may be sent and summed in bfloat16 or wider, within the bound.
A program may use at most 192 MiB of HBM per device.

v0:
```python
import math

import jax
import jax.numpy as jnp
from jax import lax
from jax.sharding import PartitionSpec as P

ridge_value = 0.5


def with_ridge(block, first_row):
    row_ids = lax.broadcasted_iota(jnp.int32, block.shape, 0) + first_row
    col_ids = lax.broadcasted_iota(jnp.int32, block.shape, 1)
    return block + jnp.where(row_ids == col_ids, ridge_value, 0.0).astype(jnp.float32)


def on_device(ex_grads, tgt_grads, projection, example_weight):
    ex_rows = ex_grads.shape[0]
    columns = projection.shape[1]
    param_total = lax.axis_size("param")
    param_pos = lax.axis_index("param")
    replica_pos = lax.axis_index("dp")
    stacked = jnp.concatenate([ex_grads, tgt_grads], axis=0)
    contract_rows = (((0,), (1,)), ((), ()))
    feature_block = lax.psum_scatter(
        lax.dot_general(projection, stacked, contract_rows, preferred_element_type=jnp.float32),
        "param",
        scatter_dimension=0,
        tiled=True,
    )
    local_features = feature_block.astype(jnp.bfloat16)
    example_part = local_features[:, :ex_rows]
    contract_first = (((0,), (0,)), ((), ()))
    partial_value = lax.dot_general(
        local_features,
        lax.all_gather(example_part, "dp", axis=1, tiled=True),
        contract_first,
        preferred_element_type=jnp.float32,
    )
    examples = partial_value.shape[1]
    summed = lax.psum(partial_value, "param")
    kernel_block = with_ridge(summed[:ex_rows] / columns, replica_pos * ex_rows)
    kernel = lax.all_gather(kernel_block, "dp", axis=0, tiled=True)
    cross_terms = summed[ex_rows:] / columns
    factor = jnp.linalg.cholesky(kernel)
    forward = jax.scipy.linalg.solve_triangular(factor, cross_terms.T, lower=True)
    solved = jax.scipy.linalg.solve_triangular(factor, forward, lower=True, trans=1)
    block_cols = examples // param_total
    chosen = lax.dynamic_slice_in_dim(solved.T, param_pos * block_cols, block_cols, 1)
    return chosen * math.sqrt(columns) * example_weight[None, :]


def solution(mesh):
    placed = (P("dp", "param"), P("dp", "param"), P("param", None), P("param"))
    return jax.shard_map(
        on_device, mesh=mesh, in_specs=placed, out_specs=P("dp", "param"), check_vma=False
    )
```

profile of v0, /device:TPU:0, one launch (start us, length us, event | category | flops | bytes accessed | tf_op | source)
XLA Modules:
  0.0 462.8 jit_solution(8862410163447170017)
XLA Ops:
  6.5 10.7 %convolution_bitcast_fusion = f32[4096,352]{0,1:T(8,128)} fusion(bf16[1280,4096]{1,0:T(8,128)(2,1)} %param.6, bf16[256,1280]{1,0:T(8,128)(2,1)} %param.5, bf16[96,1280]{1,0:T(8,128)(2,1)} %param.4), kind=kOutput, calls=%fused_computation.2 | convolution fusion | flops 3692789760 | bytes 17154048 | tf_op jit(solution)/shard_map/dot_general | solution.py:26
  17.3 57.3 %reduce-scatter.2.cloned.1.call-done = f32[1024,352]{0,1:T(8,128)} async-done(((f32[4096,352]{0,1:T(8,128)}), f32[1024,352]{0,1:T(8,128)}) %reduce-scatter.2.cloned.1.call-update) | async-done | bytes 1441808 | tf_op jit(solution)/shard_map/reduce_scatter | solution.py:25
  74.6 1.5 convert_element_type.3
  76.1 0.7 slice.254
  76.9 44.3 %all-gather.3.cloned.1.call-done = bf16[1024,768]{0,1:T(8,128)(2,1)} async-done(((bf16[1024,96]{0,1:T(8,128)(2,1)}), bf16[1024,768]{0,1:T(8,128)(2,1)}) %all-gather.3.cloned.1.call-update) | async-done | bytes 1572880 | tf_op jit(solution)/shard_map/all_gather | solution.py:36
  121.2 3.2 fusion.85
  124.4 35.1 %all-reduce.3.cloned.1.call-done = f32[352,768]{1,0:T(8,128)} async-done(((f32[352,768]{1,0:T(8,128)}), f32[352,768]{1,0:T(8,128)}) %all-reduce.3.cloned.1.call-update) | async-done | bytes 1081360 | tf_op jit(solution)/shard_map/psum | solution.py:41
  159.6 1.8 fusion.37
  161.4 0.6 iota_multiply_fusion
  162.0 1.2 fusion.4
  163.2 50.6 %all-gather.5.cloned.1.call-done = f32[768,768]{1,0:T(8,128)} async-done(((f32[96,768]{1,0:T(8,128)}), f32[768,768]{1,0:T(8,128)}) %all-gather.5.cloned.1.call-update) | async-done | bytes 2359312 | tf_op jit(solution)/shard_map/all_gather | solution.py:43
  213.8 3.6 copy.7
  217.4 2.0 fusion
  219.4 1.4 copy-done.2
  220.8 11.7 %cholesky.165 = f32[128,128]{1,0:T(8,128)S(1)} custom-call(f32[128,128]{1,0:T(8,128)S(1)} %cholesky.424), custom_call_target="Cholesky" | custom-call | tf_op jit(solution)/shard_map/jit(cholesky)/cholesky | solution.py:45
  232.7 9.8 %custom-call.50 = f32[1,128,128]{1,2,0:T(8,128)S(1)} custom-call(f32[1,128,128]{2,1,0:T(8,128)S(1)} %get-tuple-element.38), custom_call_target="InvertDiagBlocksLowerTriangular" | custom-call | tf_op jit(solution)/shard_map/jit(cholesky)/cholesky | solution.py:45
  242.5 1.4 constant_dynamic-update-slice_fusion.20
  243.9 1.4 convolution_subtract_fusion
  245.3 0.6 cholesky.428
  246.0 12.5 %cholesky.188 = f32[128,128]{1,0:T(8,128)S(1)} custom-call(f32[128,128]{1,0:T(8,128)} %cholesky.428), custom_call_target="Cholesky" | custom-call | tf_op jit(solution)/shard_map/jit(cholesky)/cholesky | solution.py:45
  258.5 0.6 select_reduce_fusion.4
  259.2 10.8 %custom-call.51 = f32[1,128,128]{1,2,0:T(8,128)S(1)} custom-call(f32[1,128,128]{2,1,0:T(8,128)} %get-tuple-element.35), custom_call_target="InvertDiagBlocksLowerTriangular" | custom-call | tf_op jit(solution)/shard_map/jit(cholesky)/cholesky | solution.py:45
  270.0 0.4 convolution_dynamic-update-slice_fusion
  270.3 1.5 convolution_subtract_fusion.1
  271.9 11.7 %cholesky.354 = f32[128,128]{1,0:T(8,128)S(1)} custom-call(f32[128,128]{1,0:T(8,128)S(1)} %cholesky.433), custom_call_target="Cholesky" | custom-call | tf_op jit(solution)/shard_map/jit(cholesky)/cholesky | solution.py:45
  283.6 9.8 %custom-call.52 = f32[1,128,128]{1,2,0:T(8,128)S(1)} custom-call(f32[1,128,128]{2,1,0:T(8,128)S(1)} %get-tuple-element.32), custom_call_target="InvertDiagBlocksLowerTriangular" | custom-call | tf_op jit(solution)/shard_map/jit(cholesky)/cholesky | solution.py:45
  293.8 1.6 convolution_subtract_fusion.2
  295.3 12.1 %cholesky.373 = f32[128,128]{1,0:T(8,128)S(1)} custom-call(f32[128,128]{1,0:T(8,128)S(1)} %cholesky.438), custom_call_target="Cholesky" | custom-call | tf_op jit(solution)/shard_map/jit(cholesky)/cholesky | solution.py:45
  307.5 9.8 %custom-call.53 = f32[1,128,128]{1,2,0:T(8,128)S(1)} custom-call(f32[1,128,128]{2,1,0:T(8,128)S(1)} %get-tuple-element.29), custom_call_target="InvertDiagBlocksLowerTriangular" | custom-call | tf_op jit(solution)/shard_map/jit(cholesky)/cholesky | solution.py:45
  317.5 1.5 convolution_subtract_fusion.11
  319.1 11.7 %cholesky.392 = f32[128,128]{1,0:T(8,128)S(1)} custom-call(f32[128,128]{1,0:T(8,128)S(1)} %cholesky.443), custom_call_target="Cholesky" | custom-call | tf_op jit(solution)/shard_map/jit(cholesky)/cholesky | solution.py:45
  330.8 9.8 %custom-call.54 = f32[1,128,128]{1,2,0:T(8,128)S(1)} custom-call(f32[1,128,128]{2,1,0:T(8,128)S(1)} %get-tuple-element.26), custom_call_target="InvertDiagBlocksLowerTriangular" | custom-call | tf_op jit(solution)/shard_map/jit(cholesky)/cholesky | solution.py:45
  340.8 1.3 convolution_subtract_fusion.14
  342.1 11.9 %cholesky.410 = f32[128,128]{1,0:T(8,128)S(1)} custom-call(f32[128,128]{1,0:T(8,128)S(1)} %convolution_subtract_fusion.14), custom_call_target="Cholesky" | custom-call | tf_op jit(solution)/shard_map/jit(cholesky)/cholesky | solution.py:45
  354.0 0.7 compare_reduce_fusion.3
  354.8 0.6 compare_reduce_fusion.2
  355.4 0.7 compare_reduce_fusion.1
  356.1 0.7 compare_reduce_fusion
  356.8 0.7 compare_reduce_fusion.4
  361.2 1.6 select_select_fusion
  362.8 20.5 %while.1 = (s32[]{:T(128)}, f32[768,768]{1,0:T(8,128)}, s32[6,2]{0,1:T(2,128)S(1)}, f32[6,128,128]{2,1,0:T(8,128)}, s32[]{:T(128)}) while((s32[]{:T(128)}, f32[768,768]{1,0:T(8,128)}, s32[6,2]{0,1:T(2,128)S(1)}, f32[6,128,128]{2,1,0:T(8,128)}, s32[]{:T(128)}) %tuple.37), condition=%wide.while_cond, body=%wide.while_body.sunk | while | flops 2 | bytes 132205 | solution.py:47
  362.9 0.5 fusion.106
  363.4 2.8 bitcast_dynamic-update-slice_fusion.2
  366.3 0.5 fusion.106
  366.8 2.8 bitcast_dynamic-update-slice_fusion.2
  369.7 0.5 fusion.106
  370.2 2.8 bitcast_dynamic-update-slice_fusion.2
  373.1 0.5 fusion.106
  373.7 2.8 bitcast_dynamic-update-slice_fusion.2
  376.6 0.5 fusion.106
  377.1 2.8 bitcast_dynamic-update-slice_fusion.2
  380.0 0.5 fusion.106
  380.5 2.8 bitcast_dynamic-update-slice_fusion.2
  383.3 59.9 %custom-call.55 = f32[6,128,128]{1,2,0:T(8,128)S(1)} custom-call(f32[6,128,128]{2,1,0:T(8,128)} %get-tuple-element.12), custom_call_target="InvertDiagBlocksLowerTriangular" | custom-call | tf_op jit(solution)/shard_map/jit(_solve_triangular)/triangular_solve | solution.py:47
  443.5 1.2 convolution_subtract_fusion.13
  445.0 1.5 convolution_subtract_fusion.10
  446.9 0.8 convolution_subtract_fusion.9
  448.0 1.0 convolution_subtract_fusion.8
  449.4 1.3 convolution_subtract_fusion.7
  451.8 0.4 convolution_subtract_fusion.6
  452.5 0.5 convolution_subtract_fusion.5
  453.3 0.6 convolution_subtract_fusion.4
  454.2 0.7 convolution_subtract_fusion.3
  455.3 0.8 multiply_bitcast_fusion
  (62 shorter events, 5.6 us)
Async XLA Ops:
  6.5 68.1 %reduce-scatter.2.cloned.1.call-start = ((), (), s32[]{:S(2)}) async-start(), calls=%async_computation.1 | async-start | bytes 7208960 | tf_op jit(solution)/shard_map/reduce_scatter | solution.py:25
  17.2 103.9 %all-gather.3.cloned.1.call-start = ((), (), s32[]{:S(2)}) async-start(), calls=%async_computation.2 | async-start | bytes 1769472 | tf_op jit(solution)/shard_map/all_gather | solution.py:36
  76.8 85.2 %copy-start.3 = (f32[192]{0:T(256)S(1)}, f32[192]{0:T(256)}, u32[]{:S(2)}) copy-start(f32[192]{0:T(256)} %param.7) | copy-start | bytes 2308
  76.8 82.7 %all-reduce.3.cloned.1.call-start = ((), (), s32[]{:S(2)}) async-start(), calls=%async_computation.3 | async-start | bytes 2162688 | tf_op jit(solution)/shard_map/psum | solution.py:41
  124.4 89.4 %all-gather.5.cloned.1.call-start = ((), (), s32[]{:S(2)}) async-start(), calls=%async_computation.4 | async-start | bytes 2654208 | tf_op jit(solution)/shard_map/all_gather | solution.py:43
  213.8 3.6 copy-start
  219.4 1.4 copy-start.2
  361.2 1.6 copy-start.4
  383.3 63.6 %copy-start.1 = (f32[768,768]{1,0:T(8,128)S(1)}, f32[768,768]{1,0:T(8,128)}, u32[]{:S(2)}) copy-start(f32[768,768]{1,0:T(8,128)} %get-tuple-element.104) | copy-start | bytes 7077892
Sparse Core Ops, SparseCore 0:
  17.4 57.2 reduce-scatter.1
  77.0 44.1 all-gather.2
  124.5 35.0 all-reduce.2
  161.6 52.1 all-gather.4
where the time goes:
time: 467 us; the launch traced here: 463 us
  other arithmetic  195 us (42%)
  waiting for transfers between devices  187 us (40%)
  matrix products  35.4 us (8%)
  local copies, waits for them, and re-layouts  27.1 us (6%)
  between operations  17.6 us (4%)
    another operation x22, other arithmetic, on_device(): factor = jnp.linalg.cholesky(kernel)  126 us
    another operation x3, other arithmetic, on_device(): jax.scipy.linalg.solve_triangular(factor, forward, lower=True, trans=1)  62.1 us
    reduce_scatter x1, waiting for transfers between devices, on_device(): lax.psum_scatter(lax.dot_general(projection, stacked, contract_rows, pref...  57.3 us
    all_gather x1, waiting for transfers between devices, on_device(): kernel = lax.all_gather(kernel_block, 'dp', axis=0, tiled=True)  50.6 us
    all_gather x1, waiting for transfers between devices, on_device(): lax.all_gather(example_part, 'dp', axis=1, tiled=True)  44.3 us
    psum x1, waiting for transfers between devices, on_device(): summed = lax.psum(partial_value, 'param')  35.1 us
    another operation x18, local copies, waits for them, and re-layouts  20.4 us
    dot_general x1, matrix products, on_device(): lax.dot_general(projection, stacked, contract_rows, preferred_element_typ...  10.7 us
  transfers between devices with their start and end apart: 4, of which 4 were waited for; matrix products, arithmetic and copies ran while one was open for 0% of the time, Pallas kernels for 0%

commit v1 on v0

v1 whole, which is shorter than its diff:
```python
import functools
import math

import jax
import jax.numpy as jnp
from jax import lax
from jax.experimental import pallas as pl
from jax.experimental.pallas import tpu as pltpu
from jax.sharding import PartitionSpec as P

ridge_value = 0.5
LANES = 128
GROUP = 8


def dot32(a, b):
    return jnp.dot(a, b, preferred_element_type=jnp.float32, precision=lax.Precision.HIGHEST)


def invert_block(block):
    size = block.shape[0]
    groups = size // GROUP
    rows = [block[GROUP * i : GROUP * (i + 1), :] for i in range(groups)]
    shape = (GROUP, size)
    sub = lax.broadcasted_iota(jnp.int32, shape, 0)
    lane = lax.broadcasted_iota(jnp.int32, shape, 1)

    def lane_splat(x, c):
        return jnp.broadcast_to(x[:, c : c + 1], shape)

    def row_splat(x, j):
        return jnp.broadcast_to(x[j : j + 1, :], shape)

    for g in range(groups):
        base = GROUP * g
        panel = rows[g]
        cols = [lane_splat(panel, base + j) for j in range(GROUP)]
        in_group = (lane >= base) & (lane < base + GROUP)
        panel = jnp.where(in_group, jnp.where(sub + base == lane, 1.0, 0.0), panel)
        for j in range(GROUP):
            inv = 1.0 / row_splat(cols[j], j)
            mult = jnp.where(sub == j, 1.0 - inv, cols[j] * inv)
            for c in range(j + 1, GROUP):
                cols[c] = cols[c] - mult * row_splat(cols[c], j)
            panel = panel - mult * row_splat(panel, j)
        spread = [row_splat(panel, j) for j in range(GROUP)]
        order = list(range(g + 1, groups)) + list(range(g))
        for i in order:
            acc = jnp.where(in_group, 0.0, rows[i])
            for j in range(GROUP):
                acc = acc - lane_splat(rows[i], base + j) * spread[j]
            rows[i] = acc
        rows[g] = panel
    return jnp.concatenate(rows, axis=0)


def solve_kernel(columns, kernel_ref, cross_ref, weight_ref, out_ref, a_ref, b_ref, inv_ref):
    n = kernel_ref.shape[0]
    blocks = n // LANES
    diag = lax.broadcasted_iota(jnp.int32, (LANES, n), 0)
    col_ids = lax.broadcasted_iota(jnp.int32, (LANES, n), 1)
    for i in range(blocks):
        part = kernel_ref[i * LANES : (i + 1) * LANES, :] / columns
        a_ref[i * LANES : (i + 1) * LANES, :] = part + jnp.where(diag + i * LANES == col_ids, ridge_value, 0.0)
    b_ref[...] = cross_ref[...] / columns

    def step(k, carry):
        at = pl.multiple_of(k * LANES, LANES)
        inv_ref[...] = invert_block(a_ref[pl.ds(at, LANES), pl.ds(at, LANES)])
        for kk in range(blocks):

            @pl.when(k == kk)
            def _():
                here = slice(kk * LANES, (kk + 1) * LANES)
                rest = slice((kk + 1) * LANES, n)
                inverse = inv_ref[...]
                z = dot32(b_ref[:, here], inverse)
                b_ref[:, here] = z
                if kk + 1 < blocks:
                    panel = a_ref[here, rest]
                    w = dot32(a_ref[rest, here], inverse)
                    a_ref[rest, here] = w
                    a_ref[rest, rest] = a_ref[rest, rest] - dot32(w, panel)
                    b_ref[:, rest] = b_ref[:, rest] - dot32(z, panel)

        return carry

    lax.fori_loop(0, blocks, step, 0)
    for k in range(blocks - 2, -1, -1):
        here = slice(k * LANES, (k + 1) * LANES)
        rest = slice((k + 1) * LANES, n)
        b_ref[:, here] = b_ref[:, here] - dot32(b_ref[:, rest], a_ref[rest, here])
    out_ref[...] = b_ref[...] * math.sqrt(columns) * weight_ref[...]


def solve(kernel, cross, weight, columns):
    n = kernel.shape[0]
    rows = cross.shape[0]
    return pl.pallas_call(
        functools.partial(solve_kernel, columns),
        out_shape=jax.ShapeDtypeStruct((rows, n), jnp.float32),
        in_specs=[pl.BlockSpec(memory_space=pltpu.VMEM)] * 3,
        out_specs=pl.BlockSpec(memory_space=pltpu.VMEM),
        scratch_shapes=[
            pltpu.VMEM((n, n), jnp.float32),
            pltpu.VMEM((rows, n), jnp.float32),
            pltpu.VMEM((LANES, LANES), jnp.float32),
        ],
    )(kernel, cross, weight)


def on_device(ex_grads, tgt_grads, projection, example_weight):
    ex_rows = ex_grads.shape[0]
    columns = projection.shape[1]
    param_total = lax.axis_size("param")
    param_pos = lax.axis_index("param")
    stacked = jnp.concatenate([ex_grads, tgt_grads], axis=0)
    contract_rows = (((0,), (1,)), ((), ()))
    feature_block = lax.psum_scatter(
        lax.dot_general(projection, stacked, contract_rows, preferred_element_type=jnp.float32),
        "param",
        scatter_dimension=0,
        tiled=True,
    )
    local_features = feature_block.astype(jnp.bfloat16)
    example_part = local_features[:, :ex_rows]
    contract_first = (((0,), (0,)), ((), ()))
    partial_value = lax.dot_general(
        local_features,
        lax.all_gather(example_part, "dp", axis=1, tiled=True),
        contract_first,
        preferred_element_type=jnp.float32,
    )
    examples = partial_value.shape[1]
    summed = lax.psum(partial_value, "param")
    kernel = lax.all_gather(summed[:ex_rows], "dp", axis=0, tiled=True)
    block_cols = examples // param_total
    scaled = solve(kernel, summed[ex_rows:], jnp.ones((1, examples), jnp.float32), columns)
    chosen = lax.dynamic_slice_in_dim(scaled, param_pos * block_cols, block_cols, 1)
    return chosen * example_weight[None, :]


def solution(mesh):
    placed = (P("dp", "param"), P("dp", "param"), P("param", None), P("param"))
    return jax.shard_map(
        on_device, mesh=mesh, in_specs=placed, out_specs=P("dp", "param"), check_vma=False
    )
```

time: 467 us -> 261 us (0.56)
  other arithmetic: 195 us -> 2.59 us
  Pallas kernels: 0 us -> 37.8 us
  matrix products: 35.4 us -> 13.8 us
  local copies, waits for them, and re-layouts: 27.1 us -> 5.84 us
    another operation x25 -> x0, other arithmetic: 188 us -> none  [the longest x22 126 us: on_device(): factor = jnp.linalg.cholesky(kernel)]
    pallas_call x0 -> x1, Pallas kernels: none -> 37.8 us  [solve(): pl.pallas_call(functools.partial(solve_kernel, columns), out_shape=jax.Sh...]
    another operation x32 -> x0, matrix products: 21.6 us -> none  [the longest x10 9.79 us: on_device(): factor = jnp.linalg.cholesky(kernel)]
    another operation x27 -> x0, local copies, waits for them, and re-layouts: 21.3 us -> none
  transfers between devices with their start and end apart: 4 -> 4, of which waited for: 4 -> 4; matrix products, arithmetic and copies ran while one was open for 0% -> 1% of each run, Pallas kernels for 0% -> 0%
where the time goes in v1:
time: 261 us
  waiting for transfers between devices  187 us (72%)
  Pallas kernels  37.8 us (14%)
  matrix products  13.8 us (5%)
  between operations  13.2 us (5%)
  local copies, waits for them, and re-layouts  5.84 us (2%)
    reduce_scatter x1, waiting for transfers between devices, on_device(): lax.psum_scatter(lax.dot_general(projection, stacked, contract_rows, pref...  57.3 us
    all_gather x1, waiting for transfers between devices, on_device(): kernel = lax.all_gather(summed[:ex_rows], 'dp', axis=0, tiled=True)  50.4 us
    all_gather x1, waiting for transfers between devices, on_device(): lax.all_gather(example_part, 'dp', axis=1, tiled=True)  44.3 us
    pallas_call x1, Pallas kernels, solve(): pl.pallas_call(functools.partial(solve_kernel, columns), out_shape=jax.Sh...  37.8 us
    psum x1, waiting for transfers between devices, on_device(): summed = lax.psum(partial_value, 'param')  35 us
    dot_general x1, matrix products, on_device(): lax.dot_general(projection, stacked, contract_rows, preferred_element_typ...  10.7 us
  transfers between devices with their start and end apart: 4, of which 4 were waited for; matrix products, arithmetic and copies ran while one was open for 1% of the time, Pallas kernels for 0%

profile of v1, /device:TPU:0, one launch (start us, length us, event | category | flops | bytes accessed | tf_op | source)
XLA Modules:
  0.0 260.7 jit_solution(2558660681553320471)
XLA Ops:
  6.5 0.0 reduce-scatter.2.cloned.1.call-start
  6.5 10.7 %convolution_bitcast_fusion = f32[4096,352]{0,1:T(8,128)} fusion(bf16[1280,4096]{1,0:T(8,128)(2,1)} %param.6, bf16[256,1280]{1,0:T(8,128)(2,1)} %param.5, bf16[96,1280]{1,0:T(8,128)(2,1)} %param.4), kind=kOutput, calls=%fused_computation | convolution fusion | flops 3692789760 | bytes 17154048 | tf_op jit(solution)/shard_map/dot_general | solution.py:120
  17.2 0.0 reduce-scatter.2.cloned.1.call-update
  17.2 0.0 all-gather.3.cloned.1.call-start
  17.3 57.3 %reduce-scatter.2.cloned.1.call-done = f32[1024,352]{0,1:T(8,128)} async-done(((f32[4096,352]{0,1:T(8,128)}), f32[1024,352]{0,1:T(8,128)}) %reduce-scatter.2.cloned.1.call-update) | async-done | bytes 1441808 | tf_op jit(solution)/shard_map/reduce_scatter | solution.py:119
  74.6 1.5 convert_element_type.3
  76.1 0.7 slice.12
  76.8 0.0 all-gather.3.cloned.1.call-update
  76.8 0.0 all-reduce.2.cloned.1.call-start
  76.9 44.3 %all-gather.3.cloned.1.call-done = bf16[1024,768]{0,1:T(8,128)(2,1)} async-done(((bf16[1024,96]{0,1:T(8,128)(2,1)}), bf16[1024,768]{0,1:T(8,128)(2,1)}) %all-gather.3.cloned.1.call-update) | async-done | bytes 1572880 | tf_op jit(solution)/shard_map/all_gather | solution.py:130
  121.2 3.1 %fusion.4 = f32[352,768]{1,0:T(8,128)} fusion(bf16[1024,352]{0,1:T(8,128)(2,1)S(1)} %convert_element_type.3, bf16[1024,768]{0,1:T(8,128)(2,1)} %all-gather.3.cloned.1.call-done), kind=kOutput, calls=%fused_computation.6 | convolution fusion | flops 553648128 | bytes 3375104 | tf_op jit(solution)/shard_map/dot_general | solution.py:128
  124.3 0.0 all-reduce.2.cloned.1.call-update
  124.3 0.2 all-gather.5.cloned.1.call-start
  124.6 35.0 %all-reduce.2.cloned.1.call-done = f32[352,768]{1,0:T(8,128)} async-done(((f32[352,768]{1,0:T(8,128)}), f32[352,768]{1,0:T(8,128)}) %all-reduce.2.cloned.1.call-update) | async-done | bytes 1081360 | tf_op jit(solution)/shard_map/psum | solution.py:135
  159.6 1.7 slice.13
  161.3 0.0 all-gather.5.cloned.1.call-update
  161.3 2.1 slice.14.cross_ref
  163.4 50.4 %all-gather.5.cloned.1.call-done.kernel_ref = f32[768,768]{1,0:T(8,128)} async-done(((f32[96,768]{1,0:T(8,128)}), f32[768,768]{1,0:T(8,128)}) %all-gather.5.cloned.1.call-update) | async-done | bytes 2359312 | tf_op jit(solution)/shard_map/all_gather | solution.py:136
  213.8 0.6 broadcast_in_dim.4.weight_ref
  214.4 0.0 copy-start
  214.4 37.8 %shard_map.46 = f32[256,768]{1,0:T(8,128)} custom-call(f32[768,768]{1,0:T(8,128)} %all-gather.5.cloned.1.call-done.kernel_ref, f32[256,768]{1,0:T(8,128)} %slice.14.cross_ref, f32[1,768]{1,0:T(1,128)} %broadcast_in_dim.4.weight_ref), custom_call_target="tpu_custom_call" | custom-call | tf_op jit(solution)/shard_map/pallas_call | solution.py:99
  252.2 0.0 copy-done
  252.2 1.1 dynamic-slice_multiply_fusion
  253.3 0.8 copy.7
Async XLA Ops:
  6.5 68.1 %reduce-scatter.2.cloned.1.call-start = ((), (), s32[]{:S(2)}) async-start(), calls=%async_computation.1 | async-start | bytes 7208960 | tf_op jit(solution)/shard_map/reduce_scatter | solution.py:119
  17.2 103.9 %all-gather.3.cloned.1.call-start = ((), (), s32[]{:S(2)}) async-start(), calls=%async_computation.2 | async-start | bytes 1769472 | tf_op jit(solution)/shard_map/all_gather | solution.py:130
  76.8 82.7 %all-reduce.2.cloned.1.call-start = ((), (), s32[]{:S(2)}) async-start(), calls=%async_computation.3 | async-start | bytes 2162688 | tf_op jit(solution)/shard_map/psum | solution.py:135
  124.3 89.4 %all-gather.5.cloned.1.call-start = ((), (), s32[]{:S(2)}) async-start(), calls=%async_computation.4 | async-start | bytes 2654208 | tf_op jit(solution)/shard_map/all_gather | solution.py:136
  214.4 37.9 %copy-start = (f32[192]{0:T(256)S(1)}, f32[192]{0:T(256)}, u32[]{:S(2)}) copy-start(f32[192]{0:T(256)} %param.7) | copy-start | bytes 2308
Sparse Core Ops, SparseCore 0:
  17.4 57.2 reduce-scatter.1
  77.0 44.1 all-gather.2
  124.5 35.0 all-reduce.1
  161.6 52.1 all-gather.4

commit v2 on v1

--- a/solution.py
+++ b/solution.py
@@ -54,15 +54,196 @@
     return jnp.concatenate(rows, axis=0)
 
 
-def solve_kernel(columns, kernel_ref, cross_ref, weight_ref, out_ref, a_ref, b_ref, inv_ref):
+def gather_kernel(own_ref, send_ref, out_ref, recv_ref, rs_send, rs_recv, send_sem, recv_sem):
+    parts, count = out_ref.shape[0], out_ref.shape[1]
+    line, pairs = count // 2, parts // 2
+    d, p = lax.axis_index("dp"), lax.axis_index("param")
+    a, b = d // 2, d % 2
+    y, c = p // 2, p % 2
+
+    barrier = pltpu.get_barrier_semaphore()
+
+    def greet(dd, pp):
+        pl.semaphore_signal(
+            barrier, inc=1, device_id={"dp": dd, "param": pp}, device_id_type=pl.DeviceIdType.MESH
+        )
+
+    for s in range(1, parts):
+        greet(d, (p + s) % parts)
+    greet(2 * a + (1 - b), p)
+    greet(2 * ((a + 1) % line) + b, p)
+    greet(2 * ((a + line - 1) % line) + b, p)
+    pl.semaphore_wait(barrier, parts + 2)
+
+    def scatter(s):
+        q = (p + s) % parts
+        return pltpu.make_async_remote_copy(
+            src_ref=send_ref.at[q],
+            dst_ref=recv_ref.at[s - 1],
+            send_sem=rs_send.at[s - 1],
+            recv_sem=rs_recv.at[s - 1],
+            device_id={"dp": d, "param": q},
+            device_id_type=pl.DeviceIdType.MESH,
+        )
+
+    for s in range(1, parts):
+        scatter(s).start()
+    for s in range(1, parts):
+        scatter(s).wait_recv()
+    total = own_ref[p]
+    for s in range(1, parts):
+        total = total + recv_ref[s - 1].astype(jnp.float32)
+    out_ref[p, d] = total.astype(out_ref.dtype)
+
+    def plane(first):
+        sent = []
+
+        def copy(i, sp, sd, dd, pp):
+            return pltpu.make_async_remote_copy(
+                src_ref=out_ref.at[sp, sd],
+                dst_ref=out_ref.at[sp, sd],
+                send_sem=send_sem.at[i],
+                recv_sem=recv_sem.at[sp, sd],
+                device_id={"dp": dd, "param": pp},
+                device_id_type=pl.DeviceIdType.MESH,
+            )
+
+        def send(cond, *args):
+            i = len(sent)
+            sent.append((cond, args))
+            if cond is None:
+                copy(i, *args).start()
+            else:
+
+                @pl.when(cond)
+                def _():
+                    copy(i, *args).start()
+
+        def arrive(cond, sp, sd):
+            wait = copy(0, sp, sd, d, p ^ 1).wait_recv
+            if cond is None:
+                wait()
+            else:
+                pl.when(cond)(wait)
+
+        def to_core(cond, sp, sd):
+            send(cond, sp, sd, d, 2 * y + (1 - c))
+
+        def to_pair(cond, sp, sd):
+            send(cond, sp, sd, 2 * a + (1 - b), p)
+
+        def to_rows(cond, sp, sd):
+            for t in range(1, pairs):
+                send(cond, sp, sd, d, 2 * ((y + t) % pairs) + c)
+
+        def ring(s):
+            if s == 0:
+                return [(None, a, 0)]
+            return [(a - s >= 0, a - s, -1), (a + s < line, a + s, 1)]
+
+        def line_block(s):
+            for cond, at, sign in ring(s):
+                sd = 2 * at + b
+                if sign:
+                    arrive(cond, p, sd)
+                    onward = a - sign
+                    ok = jnp.logical_and(cond, jnp.logical_and(onward >= 0, onward < line))
+                    send(ok, p, sd, 2 * onward + b, p)
+                else:
+                    send(a + 1 < line, p, sd, 2 * (a + 1) + b, p)
+                    send(a >= 1, p, sd, 2 * (a - 1) + b, p)
+                to_pair(cond, p, sd)
+                to_rows(cond, p, sd)
+                to_core(cond, p, sd)
+
+        def second(s):
+            for cond, at, _ in ring(s):
+                if first:
+                    sd = 2 * at + (1 - b)
+                    arrive(cond, p, sd)
+                    to_rows(cond, p, sd)
+                    to_core(cond, p, sd)
+                else:
+                    sd = 2 * at + b
+                    for t in range(1, pairs):
+                        sp = 2 * ((y + t) % pairs) + c
+                        arrive(cond, sp, sd)
+                        to_pair(cond, sp, sd)
+                        to_core(cond, sp, sd)
+
+        def third(s):
+            for cond, at, _ in ring(s):
+                if first:
+                    for t in range(1, pairs):
+                        sp = 2 * ((y + t) % pairs) + c
+                        for bb in (b, 1 - b):
+                            arrive(cond, sp, 2 * at + bb)
+                            to_core(cond, sp, 2 * at + bb)
+                else:
+                    for t in range(pairs):
+                        sp = 2 * ((y + t) % pairs) + c
+                        arrive(cond, sp, 2 * at + (1 - b))
+                        to_core(cond, sp, 2 * at + (1 - b))
+
+        line_block(0)
+        for s in range(1, line):
+            line_block(s)
+            second(s - 1)
+        second(line - 1)
+        for s in range(line):
+            third(s)
+        for yy in range(pairs):
+            for dd in range(count):
+                arrive(None, 2 * yy + (1 - c), dd)
+        for i, (cond, args) in enumerate(sent):
+            wait = copy(i, *args).wait_send
+            if cond is None:
+                wait()
+            else:
+                pl.when(cond)(wait)
+
+    @pl.when(c == 0)
+    def _():
+        plane(True)
+
+    @pl.when(c == 1)
+    def _():
+        plane(False)
+
+    for s in range(1, parts):
+        scatter(s).wait_send()
+
+
+def gather_features(partial, parts, count):
+    _, rows, block = partial.shape
+    return pl.pallas_call(
+        gather_kernel,
+        out_shape=jax.ShapeDtypeStruct((parts, count, rows, block), jnp.bfloat16),
+        in_specs=[pl.BlockSpec(memory_space=pltpu.VMEM)] * 2,
+        out_specs=pl.BlockSpec(memory_space=pltpu.VMEM),
+        scratch_shapes=[
+            pltpu.VMEM((parts - 1, rows, block), jnp.bfloat16),
+            pltpu.SemaphoreType.DMA((parts - 1,)),
+            pltpu.SemaphoreType.DMA((parts - 1,)),
+            pltpu.SemaphoreType.DMA((2 * count + 2 * parts * count,)),
+            pltpu.SemaphoreType.DMA((parts, count)),
+        ],
+        compiler_params=pltpu.CompilerParams(collective_id=0, has_side_effects=True),
+    )(partial, partial.astype(jnp.bfloat16))
+
+
+def solve_kernel(columns, parts, kernel_ref, out_ref, a_ref, b_ref, inv_ref):
     n = kernel_ref.shape[0]
+    rows = b_ref.shape[0]
     blocks = n // LANES
     diag = lax.broadcasted_iota(jnp.int32, (LANES, n), 0)
     col_ids = lax.broadcasted_iota(jnp.int32, (LANES, n), 1)
     for i in range(blocks):
         part = kernel_ref[i * LANES : (i + 1) * LANES, :] / columns
         a_ref[i * LANES : (i + 1) * LANES, :] = part + jnp.where(diag + i * LANES == col_ids, ridge_value, 0.0)
-    b_ref[...] = cross_ref[...] / columns
+    first = lax.axis_index("param") * rows
+    row_ids = lax.broadcasted_iota(jnp.int32, (rows, n), 0)
+    b_ref[...] = jnp.where(row_ids + first == lax.broadcasted_iota(jnp.int32, (rows, n), 1), 1.0, 0.0)
 
     def step(k, carry):
         at = pl.multiple_of(k * LANES, LANES)
@@ -90,54 +271,59 @@
         here = slice(k * LANES, (k + 1) * LANES)
         rest = slice((k + 1) * LANES, n)
         b_ref[:, here] = b_ref[:, here] - dot32(b_ref[:, rest], a_ref[rest, here])
-    out_ref[...] = b_ref[...] * math.sqrt(columns) * weight_ref[...]
-
-
-def solve(kernel, cross, weight, columns):
+    out_ref[...] = b_ref[...]
+
+
+def inverse_rows(kernel, columns, parts):
     n = kernel.shape[0]
-    rows = cross.shape[0]
+    rows = n // parts
     return pl.pallas_call(
-        functools.partial(solve_kernel, columns),
+        functools.partial(solve_kernel, columns, parts),
         out_shape=jax.ShapeDtypeStruct((rows, n), jnp.float32),
-        in_specs=[pl.BlockSpec(memory_space=pltpu.VMEM)] * 3,
+        in_specs=[pl.BlockSpec(memory_space=pltpu.VMEM)],
         out_specs=pl.BlockSpec(memory_space=pltpu.VMEM),
         scratch_shapes=[
             pltpu.VMEM((n, n), jnp.float32),
             pltpu.VMEM((rows, n), jnp.float32),
             pltpu.VMEM((LANES, LANES), jnp.float32),
         ],
-    )(kernel, cross, weight)
+        cost_estimate=pl.CostEstimate(flops=40 * n**3, bytes_accessed=8 * n * n, transcendentals=0),
+    )(kernel)
 
 
 def on_device(ex_grads, tgt_grads, projection, example_weight):
     ex_rows = ex_grads.shape[0]
     columns = projection.shape[1]
-    param_total = lax.axis_size("param")
-    param_pos = lax.axis_index("param")
-    stacked = jnp.concatenate([ex_grads, tgt_grads], axis=0)
-    contract_rows = (((0,), (1,)), ((), ()))
-    feature_block = lax.psum_scatter(
-        lax.dot_general(projection, stacked, contract_rows, preferred_element_type=jnp.float32),
-        "param",
-        scatter_dimension=0,
-        tiled=True,
+    parts = lax.axis_size("param")
+    count = lax.axis_size("dp")
+    examples = ex_rows * count
+    partial = jnp.dot(ex_grads, projection, preferred_element_type=jnp.float32)
+    partial = partial.reshape(ex_rows, parts, columns // parts).transpose(1, 0, 2)
+    features = gather_features(partial, parts, count).reshape(parts, examples, columns // parts)
+    kernel = sum(
+        lax.dot_general(
+            features[q], features[q], (((1,), (1,)), ((), ())), preferred_element_type=jnp.float32
+        )
+        for q in range(parts)
     )
-    local_features = feature_block.astype(jnp.bfloat16)
-    example_part = local_features[:, :ex_rows]
-    contract_first = (((0,), (0,)), ((), ()))
-    partial_value = lax.dot_general(
-        local_features,
-        lax.all_gather(example_part, "dp", axis=1, tiled=True),
-        contract_first,
+    spread = features.transpose(1, 0, 2).reshape(examples, columns)
+    mixed = lax.dot_general(
+        projection, spread, (((1,), (1,)), ((), ())), preferred_element_type=jnp.float32
+    )
+    head = lax.reduce_precision(mixed, 8, 7)
+    tail = (mixed - head).astype(jnp.bfloat16)
+    cross = jnp.dot(tgt_grads, head.astype(jnp.bfloat16), preferred_element_type=jnp.float32)
+    cross = cross + jnp.dot(tgt_grads, tail, preferred_element_type=jnp.float32)
+    cross = lax.psum(cross, "param") / columns
+    chosen = inverse_rows(kernel, columns, parts)
+    scores = lax.dot_general(
+        cross,
+        chosen,
+        (((1,), (1,)), ((), ())),
+        precision=lax.Precision.HIGHEST,
         preferred_element_type=jnp.float32,
     )
-    examples = partial_value.shape[1]
-    summed = lax.psum(partial_value, "param")
-    kernel = lax.all_gather(summed[:ex_rows], "dp", axis=0, tiled=True)
-    block_cols = examples // param_total
-    scaled = solve(kernel, summed[ex_rows:], jnp.ones((1, examples), jnp.float32), columns)
-    chosen = lax.dynamic_slice_in_dim(scaled, param_pos * block_cols, block_cols, 1)
-    return chosen * example_weight[None, :]
+    return scores * math.sqrt(columns) * example_weight[None, :]
 
 
 def solution(mesh):

time: 261 us -> 143 us (0.55)
  waiting for transfers between devices: 187 us -> 0.02 us
  Pallas kernels: 37.8 us -> 84.4 us
  matrix products: 13.8 us -> 30.2 us
  local copies, waits for them, and re-layouts: 5.84 us -> 14.6 us
    all_gather x2 -> x0, waiting for transfers between devices: 94.7 us -> none  [the longest x1 50.4 us: on_device(): kernel = lax.all_gather(summed[:ex_rows], 'dp', axis=0, tiled=True)]
    reduce_scatter x1 -> x0, waiting for transfers between devices: 57.3 us -> none  [on_device(): lax.psum_scatter(lax.dot_general(projection, stacked, contract_rows, pref...]
    pallas_call x1 -> x2, Pallas kernels: 37.8 us -> 84.4 us  [the longest x1 47.5 us: gather_features(): pl.pallas_call(gather_kernel, out_shape=jax.ShapeDtypeStruct((parts, coun...]
    psum x1, waiting for transfers between devices: 35 us -> 0.01 us  [on_device(): cross = lax.psum(cross, 'param') / columns]
    dot_general x2 -> x9, matrix products: 13.8 us -> 30.2 us  [the longest x1 12.1 us: on_device(): lax.dot_general(projection, spread, (((1,), (1,)), ((), ())), preferred_e...]
    reshape x0 -> x3, local copies, waits for them, and re-layouts: none -> 11 us  [the longest x1 8.64 us: on_device(): gather_features(partial, parts, count)]
  transfers between devices with their start and end apart: 4 -> 1, of which waited for: 4 -> 0; matrix products, arithmetic and copies ran while one was open for 1% -> 8% of each run, Pallas kernels for 0% -> 26%
where the time goes in v2:
time: 143 us
  Pallas kernels  84.4 us (59%)
  matrix products  30.2 us (21%)
  local copies, waits for them, and re-layouts  14.6 us (10%)
  between operations  13.4 us (9%)
    pallas_call x1, Pallas kernels, gather_features(): pl.pallas_call(gather_kernel, out_shape=jax.ShapeDtypeStruct((parts, coun...  47.5 us
    pallas_call x1, Pallas kernels, inverse_rows(): pl.pallas_call(functools.partial(solve_kernel, columns, parts), out_shape...  36.9 us
    dot_general x1, matrix products, on_device(): lax.dot_general(projection, spread, (((1,), (1,)), ((), ())), preferred_e...  12.1 us
    reshape x1, local copies, waits for them, and re-layouts, on_device(): gather_features(partial, parts, count)  8.64 us
    dot_general x4, matrix products, on_device(): lax.dot_general(features[q], features[q], (((1,), (1,)), ((), ())), prefe...  7.16 us
    dot_general x1, matrix products, on_device(): partial = jnp.dot(ex_grads, projection, preferred_element_type=jnp.float32)  5.96 us
    slice x1, local copies, waits for them, and re-layouts, on_device(): features[q]  3.57 us
  transfers between devices with their start and end apart: 1, of which 0 were waited for; matrix products, arithmetic and copies ran while one was open for 8% of the time, Pallas kernels for 26%

profile of v2, /device:TPU:0, one launch (start us, length us, event | category | flops | bytes accessed | tf_op | source)
XLA Modules:
  0.0 142.7 jit_solution(2959396792554461489)
XLA Ops:
  6.5 0.0 copy-start
  6.5 0.0 all-reduce.2.cloned.1.call-start
  6.5 6.0 %fusion.11 = f32[96,4096]{1,0:T(8,128)S(1)} fusion(bf16[96,1280]{1,0:T(8,128)(2,1)} %param.4, bf16[1280,4096]{1,0:T(8,128)(2,1)} %param.6), kind=kOutput, calls=%fused_computation.16 | convolution fusion | flops 1006632960 | bytes 12304384 | tf_op jit(solution)/shard_map/dot_general | solution.py:300
  12.5 1.3 copy.11
  13.8 1.1 copy.12
  14.9 47.5 %shard_map.46 = bf16[4,8,96,1024]{3,2,1,0:T(8,128)(2,1)} custom-call(f32[4,96,1024]{2,1,0:T(8,128)} %bitcast.52, bf16[4,96,1024]{2,1,0:T(8,128)(2,1)} %bitcast.53), custom_call_target="tpu_custom_call" | custom-call | tf_op jit(solution)/shard_map/pallas_call | solution.py:219
  62.4 8.6 %copy.6 = bf16[4,768,1024]{1,2,0:T(8,128)(2,1)} copy(bf16[4,768,1024]{2,1,0:T(8,128)(2,1)} %bitcast.47) | data formatting | bytes 12582912 | tf_op jit(solution)/shard_map/reshape | solution.py:302
  71.0 12.1 %fusion.12 = f32[768,1280]{1,0:T(8,128)S(1)} fusion(bf16[768,4096]{0,1:T(8,128)(2,1)} %bitcast.51, bf16[1280,4096]{1,0:T(8,128)(2,1)} %param.6), kind=kOutput, calls=%fused_computation.17 | convolution fusion | flops 8053063680 | bytes 20709376 | tf_op jit(solution)/shard_map/dot_general | solution.py:310
  83.1 0.0 copy-done
  83.1 0.7 fusion.1
  83.8 1.6 %fusion.5 = f32[256,768]{0,1:T(8,128)} fusion(f32[768,256]{1,0:T(8,128)S(1)} %fusion.1, bf16[256,1280]{1,0:T(8,128)(2,1)S(1)} %copy-done, f32[768,1280]{1,0:T(8,128)S(1)} %fusion.12), kind=kOutput, calls=%fused_computation.8 | convolution fusion | flops 505479168 | bytes 6160384 | tf_op jit(solution)/shard_map/dot_general | solution.py:315
  85.4 0.0 all-reduce.2.cloned.1.call-update
  85.5 3.6 %fusion.10 = (bf16[1,8,96,1024]{3,2,1,0:T(8,128)(2,1)S(1)}, bf16[1,8,96,1024]{3,2,1,0:T(8,128)(2,1)S(1)}, bf16[1,8,96,1024]{3,2,1,0:T(8,128)(2,1)S(1)}, bf16[1,8,96,1024]{3,2,1,0:T(8,128)(2,1)S(1)}) fusion(bf16[4,8,96,1024]{3,2,1,0:T(8,128)(2,1)} %shard_map.46), kind=kLoop, calls=%fused_computation.15 | loop fusion | bytes 12582912 | tf_op jit(solution)/shard_map/slice | solution.py:305
  89.0 1.4 fusion.13
  90.5 1.4 fusion.14
  91.9 1.4 fusion.15
  93.3 2.9 %add_add_fusion.kernel_ref = f32[768,768]{1,0:T(8,128)} fusion(f32[768,768]{1,0:T(8,128)S(1)} %fusion.15, f32[768,768]{1,0:T(8,128)S(1)} %fusion.13, f32[768,768]{1,0:T(8,128)S(1)} %fusion.14, bf16[768,1024]{1,0:T(8,128)(2,1)S(1)} %bitcast.50), kind=kOutput, calls=%fused_computation.3 | convolution fusion | flops 1209729024 | bytes 11010048 | tf_op jit(solution)/shard_map/dot_general | solution.py:304
  96.2 0.0 copy-start.1
  96.2 36.9 %shard_map.47 = f32[192,768]{1,0:T(8,128)} custom-call(f32[768,768]{1,0:T(8,128)} %add_add_fusion.kernel_ref), custom_call_target="tpu_custom_call" | custom-call | flops 18119393280 | bytes 4718592 | tf_op jit(solution)/shard_map/pallas_call | solution.py:280
  133.1 0.0 copy-done.1
  133.1 0.0 all-reduce.2.cloned.1.call-done
  133.1 2.7 %convolution_multiply_fusion = f32[256,192]{0,1:T(8,128)} fusion(f32[192,768]{1,0:T(8,128)} %shard_map.47, f32[256,768]{0,1:T(8,128)} %all-reduce.2.cloned.1.call-done, f32[192]{0:T(256)S(1)} %broadcast_multiply_fusion), kind=kOutput, calls=%fused_computation.9 | convolution fusion | flops 453230592 | bytes 1573632 | tf_op jit(solution)/shard_map/dot_general | solution.py:319
  (1 shorter events, 0.0 us)
Async XLA Ops:
  6.5 76.6 %copy-start = (bf16[256,1280]{1,0:T(8,128)(2,1)S(1)}, bf16[256,1280]{1,0:T(8,128)(2,1)}, u32[]{:S(2)}) copy-start(bf16[256,1280]{1,0:T(8,128)(2,1)} %param.5) | copy-start | bytes 1966084
  6.5 126.6 %all-reduce.2.cloned.1.call-start = ((), (), s32[]{:S(2)}) async-start(), calls=%async_computation | async-start | bytes 1572864 | tf_op jit(solution)/shard_map/psum | solution.py:317
  96.2 36.9 %copy-start.1 = (f32[192]{0:T(256)S(1)}, f32[192]{0:T(256)}, u32[]{:S(2)}) copy-start(f32[192]{0:T(256)} %param.7) | copy-start | bytes 2308
Sparse Core Ops, SparseCore 0:
  85.6 33.6 all-reduce.1

commit v3 on v2

--- a/solution.py
+++ b/solution.py
@@ -55,11 +55,15 @@
 
 
 def gather_kernel(own_ref, send_ref, out_ref, recv_ref, rs_send, rs_recv, send_sem, recv_sem):
-    parts, count = out_ref.shape[0], out_ref.shape[1]
+    parts, count = lax.axis_size("param"), out_ref.shape[0]
+    block = out_ref.shape[2] // parts
     line, pairs = count // 2, parts // 2
     d, p = lax.axis_index("dp"), lax.axis_index("param")
     a, b = d // 2, d % 2
     y, c = p // 2, p % 2
+
+    def part(sp):
+        return pl.ds(pl.multiple_of(sp * block, LANES), block)
 
     barrier = pltpu.get_barrier_semaphore()
 
@@ -78,7 +82,7 @@
     def scatter(s):
         q = (p + s) % parts
         return pltpu.make_async_remote_copy(
-            src_ref=send_ref.at[q],
+            src_ref=send_ref.at[:, part(q)],
             dst_ref=recv_ref.at[s - 1],
             send_sem=rs_send.at[s - 1],
             recv_sem=rs_recv.at[s - 1],
@@ -90,18 +94,18 @@
         scatter(s).start()
     for s in range(1, parts):
         scatter(s).wait_recv()
-    total = own_ref[p]
+    total = own_ref[:, part(p)]
     for s in range(1, parts):
         total = total + recv_ref[s - 1].astype(jnp.float32)
-    out_ref[p, d] = total.astype(out_ref.dtype)
+    out_ref[d, :, part(p)] = total.astype(out_ref.dtype)
 
     def plane(first):
         sent = []
 
         def copy(i, sp, sd, dd, pp):
             return pltpu.make_async_remote_copy(
-                src_ref=out_ref.at[sp, sd],
-                dst_ref=out_ref.at[sp, sd],
+                src_ref=out_ref.at[sd, :, part(sp)],
+                dst_ref=out_ref.at[sd, :, part(sp)],
                 send_sem=send_sem.at[i],
                 recv_sem=recv_sem.at[sp, sd],
                 device_id={"dp": dd, "param": pp},
@@ -215,10 +219,11 @@
 
 
 def gather_features(partial, parts, count):
-    _, rows, block = partial.shape
+    rows, columns = partial.shape
+    block = columns // parts
     return pl.pallas_call(
         gather_kernel,
-        out_shape=jax.ShapeDtypeStruct((parts, count, rows, block), jnp.bfloat16),
+        out_shape=jax.ShapeDtypeStruct((count, rows, columns), jnp.bfloat16),
         in_specs=[pl.BlockSpec(memory_space=pltpu.VMEM)] * 2,
         out_specs=pl.BlockSpec(memory_space=pltpu.VMEM),
         scratch_shapes=[
@@ -298,18 +303,10 @@
     count = lax.axis_size("dp")
     examples = ex_rows * count
     partial = jnp.dot(ex_grads, projection, preferred_element_type=jnp.float32)
-    partial = partial.reshape(ex_rows, parts, columns // parts).transpose(1, 0, 2)
-    features = gather_features(partial, parts, count).reshape(parts, examples, columns // parts)
-    kernel = sum(
-        lax.dot_general(
-            features[q], features[q], (((1,), (1,)), ((), ())), preferred_element_type=jnp.float32
-        )
-        for q in range(parts)
-    )
-    spread = features.transpose(1, 0, 2).reshape(examples, columns)
-    mixed = lax.dot_general(
-        projection, spread, (((1,), (1,)), ((), ())), preferred_element_type=jnp.float32
-    )
+    features = gather_features(partial, parts, count).reshape(examples, columns)
+    contract_last = (((1,), (1,)), ((), ()))
+    kernel = lax.dot_general(features, features, contract_last, preferred_element_type=jnp.float32)
+    mixed = lax.dot_general(projection, features, contract_last, preferred_element_type=jnp.float32)
     head = lax.reduce_precision(mixed, 8, 7)
     tail = (mixed - head).astype(jnp.bfloat16)
     cross = jnp.dot(tgt_grads, head.astype(jnp.bfloat16), preferred_element_type=jnp.float32)

time: 143 us -> 133 us (0.930)
  local copies, waits for them, and re-layouts: 14.6 us -> 0.01 us
  matrix products: 30.2 us -> 35.2 us
    reshape x3 -> x0, local copies, waits for them, and re-layouts: 11 us -> none  [the longest x1 8.64 us: on_device(): gather_features(partial, parts, count)]
    dot_general x5 -> x2, matrix products: 19.2 us -> 22.8 us  [the longest x1 12 us: on_device(): lax.dot_general(projection, features, contract_last, preferred_element_ty...]
    slice x1 -> x0, local copies, waits for them, and re-layouts: 3.57 us -> none  [on_device(): features[q]]
    dot_general x1, matrix products: 5.96 us -> 7.41 us  [on_device(): partial = jnp.dot(ex_grads, projection, preferred_element_type=jnp.float32)]
  transfers between devices with their start and end apart: 1 -> 1, of which waited for: 0 -> 0; matrix products, arithmetic and copies ran while one was open for 8% -> 8% of each run, Pallas kernels for 26% -> 28%
where the time goes in v3:
time: 133 us
  Pallas kernels  84.1 us (63%)
  matrix products  35.2 us (26%)
  between operations  13.4 us (10%)
    pallas_call x1, Pallas kernels, gather_features(): pl.pallas_call(gather_kernel, out_shape=jax.ShapeDtypeStruct((count, rows...  47.3 us
    pallas_call x1, Pallas kernels, inverse_rows(): pl.pallas_call(functools.partial(solve_kernel, columns, parts), out_shape...  36.8 us
    dot_general x1, matrix products, on_device(): lax.dot_general(projection, features, contract_last, preferred_element_ty...  12 us
    dot_general x1, matrix products, on_device(): lax.dot_general(features, features, contract_last, preferred_element_type...  10.8 us
    dot_general x1, matrix products, on_device(): partial = jnp.dot(ex_grads, projection, preferred_element_type=jnp.float32)  7.41 us
    dot_general x1, matrix products, on_device(): lax.dot_general(cross, chosen, (((1,), (1,)), ((), ())), precision=lax.Pr...  2.68 us
  transfers between devices with their start and end apart: 1, of which 0 were waited for; matrix products, arithmetic and copies ran while one was open for 8% of the time, Pallas kernels for 28%

profile of v3, /device:TPU:0, one launch (start us, length us, event | category | flops | bytes accessed | tf_op | source)
XLA Modules:
  0.0 132.8 jit_solution(4438750222704983007)
XLA Ops:
  6.5 0.0 copy-start
  6.5 0.0 all-reduce.2.cloned.1.call-start
  6.5 7.4 %fusion.9 = (bf16[96,4096]{1,0:T(8,128)(2,1)}, f32[96,4096]{1,0:T(8,128)}) fusion(bf16[96,1280]{1,0:T(8,128)(2,1)} %param.4, bf16[1280,4096]{1,0:T(8,128)(2,1)} %param.6), kind=kOutput, calls=%fused_computation.12 | convolution fusion | flops 1007026176 | bytes 13090816 | tf_op jit(solution)/shard_map/dot_general | solution.py:305
  13.9 47.3 %shard_map.46 = bf16[8,96,4096]{2,1,0:T(8,128)(2,1)} custom-call(f32[96,4096]{1,0:T(8,128)} %get-tuple-element.6.own_ref, bf16[96,4096]{1,0:T(8,128)(2,1)} %get-tuple-element.5.send_ref), custom_call_target="tpu_custom_call" | custom-call | tf_op jit(solution)/shard_map/pallas_call | solution.py:224
  61.3 12.0 %fusion.10 = f32[768,1280]{1,0:T(8,128)S(1)} fusion(bf16[768,4096]{1,0:T(8,128)(2,1)} %bitcast.21, bf16[1280,4096]{1,0:T(8,128)(2,1)} %param.6), kind=kOutput, calls=%fused_computation.13 | convolution fusion | flops 8053063680 | bytes 20709376 | tf_op jit(solution)/shard_map/dot_general | solution.py:309
  73.3 0.0 copy-done
  73.3 0.7 fusion.1
  74.1 1.6 %fusion.5 = f32[256,768]{0,1:T(8,128)} fusion(f32[768,256]{1,0:T(8,128)S(1)} %fusion.1, bf16[256,1280]{1,0:T(8,128)(2,1)S(1)} %copy-done, f32[768,1280]{1,0:T(8,128)S(1)} %fusion.10), kind=kOutput, calls=%fused_computation.6 | convolution fusion | flops 505479168 | bytes 6160384 | tf_op jit(solution)/shard_map/dot_general | solution.py:312
  75.7 0.0 all-reduce.2.cloned.1.call-update
  75.7 10.8 %fusion.11.kernel_ref = f32[768,768]{1,0:T(8,128)} fusion(bf16[768,4096]{1,0:T(8,128)(2,1)} %bitcast.22), kind=kOutput, calls=%fused_computation.14 | convolution fusion | flops 4831838208 | bytes 8650752 | tf_op jit(solution)/shard_map/dot_general | solution.py:308
  86.5 0.0 copy-start.1
  86.5 36.8 %shard_map.47 = f32[192,768]{1,0:T(8,128)} custom-call(f32[768,768]{1,0:T(8,128)} %fusion.11.kernel_ref), custom_call_target="tpu_custom_call" | custom-call | flops 18119393280 | bytes 4718592 | tf_op jit(solution)/shard_map/pallas_call | solution.py:285
  123.3 0.0 copy-done.1
  123.3 0.0 all-reduce.2.cloned.1.call-done
  123.3 2.7 %convolution_multiply_fusion = f32[256,192]{0,1:T(8,128)} fusion(f32[192,768]{1,0:T(8,128)} %shard_map.47, f32[256,768]{0,1:T(8,128)} %all-reduce.2.cloned.1.call-done, f32[192]{0:T(256)S(1)} %broadcast_multiply_fusion), kind=kOutput, calls=%fused_computation.7 | convolution fusion | flops 453230592 | bytes 1573632 | tf_op jit(solution)/shard_map/dot_general | solution.py:316
  (1 shorter events, 0.0 us)
Async XLA Ops:
  6.5 66.8 %copy-start = (bf16[256,1280]{1,0:T(8,128)(2,1)S(1)}, bf16[256,1280]{1,0:T(8,128)(2,1)}, u32[]{:S(2)}) copy-start(bf16[256,1280]{1,0:T(8,128)(2,1)} %param.5) | copy-start | bytes 1966084
  6.5 116.8 %all-reduce.2.cloned.1.call-start = ((), (), s32[]{:S(2)}) async-start(), calls=%async_computation | async-start | bytes 1572864 | tf_op jit(solution)/shard_map/psum | solution.py:314
  86.5 36.8 %copy-start.1 = (f32[192]{0:T(256)S(1)}, f32[192]{0:T(256)}, u32[]{:S(2)}) copy-start(f32[192]{0:T(256)} %param.7) | copy-start | bytes 2308
Sparse Core Ops, SparseCore 0:
  75.8 33.6 all-reduce.1
